TPU v7x, 32 devices: a whole 2x2x4 slice. The times are simulated.
32 devices in a mesh: src: 16 (over z, y, x), hid: 2 (over core).
Axes of the slice: x: 2, y: 2, z: 4, core: 2. Of those that a mesh axis runs over, the one named last changes fastest.
Arguments:
- source_field: float32 [128, 2, 98, 128], P('src'), may hold values from -36 to 36
- hidden_gain: float32 [98], replicated, may hold values from 0.1 to 1.9
- enc_tiles: float32 [1024, 128, 128], P(('src', 'hid')), may hold values from -0.25 to 0.25
- enc_src_block: int32 [1024], P(('src', 'hid')), may hold values from 0 to 127, as said below
- enc_hid_block: int32 [1024], P(('src', 'hid')), may hold values from 0 to 63, as said below
- enc_count: int32 [32], P(('src', 'hid')), may hold values from 1 to 32, as said below
- dec_tiles: float32 [1024, 128, 128], P(('src', 'hid')), may hold values from -0.15625 to 0.15625
- dec_src_block: int32 [1024], P(('src', 'hid')), may hold values from 0 to 127, as said below
- dec_hid_block: int32 [1024], P(('src', 'hid')), may hold values from 0 to 63, as said below
- dec_count: int32 [32], P(('src', 'hid')), may hold values from 1 to 32, as said below
Outputs:
- returned: float32 [128, 2, 98, 128], P('src')
- channel_rms: float32 [98], replicated
Inputs may be any that keep to these rules, and one draw needn't show every extreme that they name: `enc_src_block`: the 32 entries starting at (s * 2 + h) * 32 lie in s * 8 to (s + 1) * 8 - 1. `enc_hid_block`: the 32 entries starting at (s * 2 + h) * 32 lie in h * 32 to (h + 1) * 32 - 1; within these entries no pair (enc_src_block, enc_hid_block) repeats. `enc_count`: entry s * 2 + h counts the live slots of that group; it equals 32 for some group. `dec_src_block`: the 32 entries starting at (s * 2 + h) * 32 lie in s * 8 to (s + 1) * 8 - 1. `dec_hid_block`: the 32 entries starting at (s * 2 + h) * 32 lie in h * 32 to (h + 1) * 32 - 1; within these entries no pair (dec_src_block, dec_hid_block) repeats. `dec_count`: entry s * 2 + h counts the live slots of that group; it equals 32 for some group.
All inputs are finite; a program needn't handle non-finite values.
Results may differ from a plain program's by a relative error of at most 0.0003.
Values sent between devices are 32-bit elements; how exact they have to be, the bound alone decides.
No kernel may reach another device: no remote copies, remote signals or barrier semaphores. Data moves between devices by JAX's collectives and lax.ppermute only.
A program may use at most 64 MiB of HBM per device.

v0:
```python
import jax
import jax.numpy as jnp
from jax import lax
from jax.sharding import PartitionSpec as P

HID_BLK = 32
GROUP = 16


HIGH = lax.Precision.HIGHEST
EPSILON = 1e-06


def normalize(total, gain, batch, channels):
    nodes, features, width = total.shape
    grouped = total.reshape(nodes, batch, channels, width)
    mean_square = jnp.mean(grouped * grouped, axis=2, keepdims=True)
    scaled = grouped * gain[None, None, :, None] * lax.rsqrt(mean_square + EPSILON)
    return scaled.reshape(nodes, features, width)


def body(
    source_field,
    hidden_gain,
    enc_tiles,
    enc_src_block,
    enc_hid_block,
    enc_count,
    dec_tiles,
    dec_src_block,
    dec_hid_block,
    dec_count,
):
    src_blocks, batch, channels, width = source_field.shape
    features = batch * channels
    flat = source_field.reshape(src_blocks, features, width)
    src_first = lax.axis_index("src") * src_blocks
    hid_first = lax.axis_index("hid") * HID_BLK
    enc_sources = enc_src_block - src_first
    enc_targets = enc_hid_block - hid_first
    dec_targets = dec_src_block - src_first
    dec_sources = dec_hid_block - hid_first
    src_range = jnp.arange(src_blocks, dtype=jnp.int32)
    hid_range = jnp.arange(HID_BLK, dtype=jnp.int32)
    slot_range = jnp.arange(GROUP, dtype=jnp.int32)

    def encode_group(step, partial_value):
        start = step * GROUP
        tiles = lax.dynamic_slice_in_dim(enc_tiles, start, GROUP, 0)
        sources = lax.dynamic_slice_in_dim(enc_sources, start, GROUP, 0)
        targets = lax.dynamic_slice_in_dim(enc_targets, start, GROUP, 0)
        alive = (start + slot_range < enc_count[0])[:, None]
        select = (sources[:, None] == src_range[None, :]).astype(jnp.float32)
        placing = (alive & (targets[:, None] == hid_range[None, :])).astype(jnp.float32)
        blocks = jnp.einsum("ts,sfc->tfc", select, flat, precision=HIGH)
        product = jnp.einsum("tfr,trc->tfc", blocks, tiles, precision=HIGH)
        return partial_value + jnp.einsum("th,tfc->hfc", placing, product, precision=HIGH)

    enc_groups = (enc_count[0] + GROUP - 1) // GROUP
    partial_value = lax.fori_loop(
        0, enc_groups, encode_group, jnp.zeros((HID_BLK, features, width), jnp.float32)
    )
    hidden = normalize(lax.psum(partial_value, "src"), hidden_gain, batch, channels)

    def fetch(start):
        sources = lax.dynamic_slice_in_dim(dec_sources, start, GROUP, 0)
        select = (sources[:, None] == hid_range[None, :]).astype(jnp.float32)
        return jnp.einsum("th,hfc->tfc", select, hidden, precision=HIGH)

    def decode_group(step, partial_back):
        start = step * GROUP
        tiles = lax.dynamic_slice_in_dim(dec_tiles, start, GROUP, 0)
        targets = lax.dynamic_slice_in_dim(dec_targets, start, GROUP, 0)
        alive = (start + slot_range < dec_count[0])[:, None]
        blocks = fetch(start)
        product = jnp.einsum("tfr,trc->tfc", blocks, tiles, precision=HIGH)
        placing = (alive & (targets[:, None] == src_range[None, :])).astype(jnp.float32)
        return partial_back + jnp.einsum("ts,tfc->sfc", placing, product, precision=HIGH)

    dec_groups = (dec_count[0] + GROUP - 1) // GROUP
    partial_back = lax.fori_loop(
        0, dec_groups, decode_group, jnp.zeros((src_blocks, features, width), jnp.float32)
    )
    total_points = src_blocks * lax.axis_size("src") * batch * width
    returned = lax.psum(partial_back, "hid")
    difference = returned - flat
    squares = jnp.sum(
        (difference * difference).reshape(src_blocks, batch, channels, width), axis=(0, 1, 3)
    )
    sums = lax.psum(squares, "src")
    channel_rms = jnp.sqrt(sums / total_points + EPSILON)
    return (returned.reshape(source_field.shape), channel_rms)


def solution(mesh):
    in_specs = (
        P("src", None, None, None),
        P(),
        P(("src", "hid"), None, None),
        P(("src", "hid")),
        P(("src", "hid")),
        P(("src", "hid")),
        P(("src", "hid"), None, None),
        P(("src", "hid")),
        P(("src", "hid")),
        P(("src", "hid")),
    )
    out_specs = (P("src", None, None, None), P())
    return jax.shard_map(body, mesh=mesh, in_specs=in_specs, out_specs=out_specs, check_vma=False)
```

profile of v0, /device:TPU:0, one launch (start us, length us, event | category | flops | bytes accessed | tf_op | source)
XLA Modules:
  0.0 276.8 jit_solution(4805491269484964007)
XLA Ops:
  7.9 2.1 copy.23
  11.0 17.4 %while.22 = (s32[]{:T(128)}, f32[32,196,128]{2,0,1:T(8,128)S(1)}, s32[]{:T(128)}, s32[1]{0:T(128)}, s32[32]{0:T(128)S(1)}, /*index=5*/s32[32]{0:T(128)S(1)}, f32...) while((s32[]{:T(128)}, f32[32,196,128]{2,0,1:T(8,128)S(1)}, ...), condition=%wide.region_1.2_spmd.clone, body=%wide.region_0.1_spmd.clone.sunk | while | flops 810042496 | bytes 23085684 | solution.py:60
  11.2 2.1 fusion.73
  13.3 3.2 %fusion.74 = f32[16,196,128]{2,1,0:T(8,128)S(1)} fusion(f32[16,196,128]{2,0,1:T(8,128)S(1)} %fusion.73, f32[32,128,128]{2,1,0:T(8,128)S(1)} %copy-done.1, s32[]{:T(128)S(6)} %select_n.24), kind=kOutput, calls=%fused_computation.7.clone.1 | convolution fusion | flops 616562688 | bytes 4259844 | tf_op jit(solution)/shard_map/while/body/tfr,trc->tfc/dot_general | solution.py:56
  17.2 2.6 convolution_add_fusion.2
  19.9 2.1 fusion.73
  22.0 3.2 %fusion.74 = f32[16,196,128]{2,1,0:T(8,128)S(1)} fusion(f32[16,196,128]{2,0,1:T(8,128)S(1)} %fusion.73, f32[32,128,128]{2,1,0:T(8,128)S(1)} %copy-done.1, s32[]{:T(128)S(6)} %select_n.24), kind=kOutput, calls=%fused_computation.7.clone.1 | convolution fusion | flops 616562688 | bytes 4259844 | tf_op jit(solution)/shard_map/while/body/tfr,trc->tfc/dot_general | solution.py:56
  25.9 2.6 convolution_add_fusion.2
  28.5 1.7 copy-done
  31.0 150.9 %all-reduce.3.cloned.1.call-done = f32[32,196,128]{2,0,1:T(8,128)} async-done(((f32[32,196,128]{2,0,1:T(8,128)}), f32[32,196,128]{2,0,1:T(8,128)}) %all-reduce.3.cloned.1.call-update) | async-done | bytes 3211280 | tf_op jit(solution)/shard_map/psum | solution.py:63
  181.9 3.6 %mul.51 = f32[32,196,128]{2,0,1:T(8,128)S(1)} multiply(f32[32,196,128]{2,0,1:T(8,128)} %all-reduce.3.cloned.1.call-done, f32[32,196,128]{2,0,1:T(8,128)} %all-reduce.3.cloned.1.call-done) | non-fusion elementwise | flops 802816 | bytes 9633792 | tf_op jit(solution)/shard_map/mul | solution.py:17
  185.8 2.2 bitcast_multiply_fusion
  188.0 0.9 broadcast_in_dim.4
  189.0 16.7 %while.23 = (s32[]{:T(128)}, f32[8,196,128]{2,0,1:T(8,128)}, s32[]{:T(128)}, s32[1]{0:T(128)}, s32[32]{0:T(128)S(1)}, /*index=5*/s32[32]{0:T(128)S(1)}, f32[32,1...) while((s32[]{:T(128)}, f32[8,196,128]{2,0,1:T(8,128)}, ...), condition=%wide.region_5.6_spmd.clone, body=%wide.region_4.5_spmd.clone.sunk | while | flops 809440000 | bytes 20677236 | solution.py:81
  189.0 1.2 fusion.82
  190.6 3.2 %fusion.83 = f32[16,196,128]{2,1,0:T(8,128)S(1)} fusion(f32[16,196,128]{2,0,1:T(8,128)S(1)} %fusion.82, f32[32,128,128]{2,1,0:T(8,128)S(1)} %copy-done.2, s32[]{:T(128)S(6)} %select_n.25), kind=kOutput, calls=%fused_computation.23.clone.1 | convolution fusion | flops 616562688 | bytes 4259844 | tf_op jit(solution)/shard_map/while/body/tfr,trc->tfc/dot_general | solution.py:76
  194.5 2.8 %fusion.85 = f32[8,196,128]{2,0,1:T(8,128)} fusion(f32[8,196,128]{2,0,1:T(8,128)} %get-tuple-element.375, f32[16,196,128]{2,1,0:T(8,128)S(1)} %fusion.83, s32[16]{0:T(128)S(1)} %dynamic_slice.39, pred[16]{0:T(512)(128)(4,1)S(1)} %fusion.84), kind=kOutput, calls=%fused_computation.27.clone.1 | convolution fusion | flops 38736128 | bytes 3211344 | tf_op jit(solution)/shard_map/while/body/ts,tfc->sfc/dot_general | solution.py:78
  197.4 1.2 fusion.82
  199.0 3.2 %fusion.83 = f32[16,196,128]{2,1,0:T(8,128)S(1)} fusion(f32[16,196,128]{2,0,1:T(8,128)S(1)} %fusion.82, f32[32,128,128]{2,1,0:T(8,128)S(1)} %copy-done.2, s32[]{:T(128)S(6)} %select_n.25), kind=kOutput, calls=%fused_computation.23.clone.1 | convolution fusion | flops 616562688 | bytes 4259844 | tf_op jit(solution)/shard_map/while/body/tfr,trc->tfc/dot_general | solution.py:76
  202.9 2.8 %fusion.85 = f32[8,196,128]{2,0,1:T(8,128)} fusion(f32[8,196,128]{2,0,1:T(8,128)} %get-tuple-element.375, f32[16,196,128]{2,1,0:T(8,128)S(1)} %fusion.83, s32[16]{0:T(128)S(1)} %dynamic_slice.39, pred[16]{0:T(512)(128)(4,1)S(1)} %fusion.84), kind=kOutput, calls=%fused_computation.27.clone.1 | convolution fusion | flops 38736128 | bytes 3211344 | tf_op jit(solution)/shard_map/while/body/ts,tfc->sfc/dot_general | solution.py:78
  205.7 17.9 %all-reduce.5.cloned.1.call-done = f32[8,196,128]{2,0,1:T(8,128)} async-done(((f32[8,196,128]{2,0,1:T(8,128)}), f32[8,196,128]{2,0,1:T(8,128)}) %all-reduce.5.cloned.1.call-update) | async-done | bytes 802832 | tf_op jit(solution)/shard_map/psum | solution.py:85
  223.6 2.5 multiply_reduce_fusion
  226.2 42.0 %psum.23 = f32[98]{0:T(128)S(1)} all-reduce(f32[98]{0:T(128)S(1)} %reduce_sum.28), channel_id=1, replica_groups=mesh['src'=16,'hid'=2] {'src'}, use_global_device_ids=true, to_apply=%region_9.10 | all-reduce | flops 98 | bytes 784 | tf_op jit(solution)/shard_map/psum | solution.py:90
  268.7 1.3 copy.24
  (43 shorter events, 6.1 us)
Async XLA Ops:
  7.2 174.7 %all-reduce.3.cloned.1.call-start = ((), (), s32[]{:S(2)}) async-start(), calls=%async_computation | async-start | bytes 6422528 | tf_op jit(solution)/shard_map/psum | solution.py:63
  11.1 2.2 copy-start.1
  19.8 2.2 copy-start.1
  28.5 1.7 copy-start
  28.5 2.4 copy-start.6
  28.5 2.5 copy-start.4
  28.5 2.5 copy-start.5
  30.2 193.3 %all-reduce.5.cloned.1.call-start = ((), (), s32[]{:S(2)}) async-start(), calls=%async_computation.1 | async-start | bytes 1605632 | tf_op jit(solution)/shard_map/psum | solution.py:85
  189.0 1.6 copy-start.2
  197.4 1.6 copy-start.2
  223.6 45.1 %copy-start.3 = (f32[8,196,128]{2,0,1:T(8,128)S(1)}, f32[8,196,128]{2,0,1:T(8,128)}, u32[]{:S(2)}) copy-start(f32[8,196,128]{2,0,1:T(8,128)} %all-reduce.5.cloned.1.call-done) | copy-start | bytes 2408452
Sparse Core Ops, SparseCore 0:
  30.3 151.5 all-reduce.2
  205.8 17.7 all-reduce.4
where the time goes:
time: 278 us; the launch traced here: 277 us
  waiting for transfers between devices  169 us (61%)
  blocking collectives  42 us (15%)
  matrix products  30 us (11%)
  between operations  15.5 us (6%)
  other arithmetic  12.4 us (4%)
  local copies, waits for them, and re-layouts  7.89 us (3%)
    psum x1, waiting for transfers between devices, body(): lax.psum(partial_value, 'src')  151 us
    psum x1, blocking collectives, body(): sums = lax.psum(squares, 'src')  42 us
    psum x1, waiting for transfers between devices, body(): returned = lax.psum(partial_back, 'hid')  17.9 us
    dot_general x2, matrix products, encode_group(): product = jnp.einsum('tfr,trc->tfc', blocks, tiles, precision=HIGH)  6.31 us
    dot_general x2, matrix products, decode_group(): product = jnp.einsum('tfr,trc->tfc', blocks, tiles, precision=HIGH)  6.31 us
    dot_general x2, matrix products, decode_group(): jnp.einsum('ts,tfc->sfc', placing, product, precision=HIGH)  5.57 us
  transfers between devices with their start and end apart: 2, of which 2 were waited for; matrix products, arithmetic and copies ran while one was open for 0% of the time, Pallas kernels for 0%

commit v1 on v0

v1 whole, which is shorter than its diff:
```python
import functools

import jax
import jax.numpy as jnp
from jax import lax
from jax.experimental import pallas as pl
from jax.experimental.pallas import tpu as pltpu
from jax.sharding import PartitionSpec as P

HID_BLK = 32
EPSILON = 1e-06
UNROLL = 4

VMEM = pltpu.MemorySpace.VMEM
SMEM = pltpu.MemorySpace.SMEM
IN_VMEM = pl.BlockSpec(memory_space=VMEM)
IN_SMEM = pl.BlockSpec(memory_space=SMEM)
ANYWHERE = pl.BlockSpec(memory_space=pl.ANY)
PARAMS = pltpu.CompilerParams(vmem_limit_bytes=24 * 1024 * 1024)


class Stream:
    def __init__(self, first, units, orders):
        self.first, self.units, self.orders = first, units, orders


def make_streams(bits, owned):
    turn = lambda k: bits[k % len(bits):] + bits[: k % len(bits)]
    streams = []
    for unit in range(owned):
        first = unit % len(bits)
        second = first + (unit + 1 == owned and owned > len(bits))
        streams.append(Stream(unit, 1, (turn(first), turn(second))))
    return streams


def split(value):
    high = value.astype(jnp.bfloat16)
    low = (value - high.astype(jnp.float32)).astype(jnp.bfloat16)
    return high, low


def tile_weights(tile):
    high, low = split(tile)
    line = jnp.concatenate([high, low], axis=1)
    return jnp.concatenate([line, line], axis=0)


def block_rows(value):
    return jnp.concatenate(split(value), axis=1)


def multiply(rows, tile):
    product = jnp.dot(rows, tile_weights(tile), preferred_element_type=jnp.float32)
    width = tile.shape[1]
    return product[:, :width] + product[:, width:]


def position_of(block, cube, streams):
    mine = lax.bitwise_and(lax.axis_index("src"), cube - 1)
    core = lax.bitwise_and(lax.axis_index("hid"), 1)
    away = lax.bitwise_xor(lax.rem(block, cube), mine)
    unit = lax.div(block, cube)
    place = jnp.int32(0)
    for stream in streams:
        depth = len(stream.orders[0])
        spot = jnp.int32(0)
        for stage in range(depth):
            bit = jnp.where(core == 0, stream.orders[0][stage], stream.orders[1][stage])
            one = lax.bitwise_and(lax.shift_right_logical(away, bit), 1)
            spot = spot + one * (1 << (depth - 1 - stage))
        here = stream.first * cube + spot * stream.units + unit - stream.first
        place = jnp.where(unit >= stream.first, here, place)
    return place


def encode_kernel(cube, streams, count, sources_in, targets_in, field_in, tiles_in, *rest):
    outs = rest[: 2 * len(streams)]
    sources, targets, field, tiles, lhs, acc, small, large, sems = rest[2 * len(streams):]
    blocks, rows = lhs.shape[0], lhs.shape[1]
    used = field.shape[0] // blocks
    groups = tiles.shape[0] // UNROLL
    copies = [pltpu.make_async_copy(sources_in, sources, small.at[1]),
              pltpu.make_async_copy(targets_in, targets, small.at[2]),
              pltpu.make_async_copy(field_in, field, large)]

    def tile_copy(g):
        span = pl.ds(g * UNROLL, UNROLL)
        return pltpu.make_async_copy(tiles_in.at[span], tiles.at[span], sems.at[g])

    for copy in copies:
        copy.start()
    for g in range(groups):
        tile_copy(g).start()
    acc[...] = jnp.zeros_like(acc)
    for copy in copies:
        copy.wait()
    pad = jnp.zeros((rows - used, field.shape[1]), jnp.float32)
    for b in range(blocks):
        lhs[b] = block_rows(jnp.concatenate([field[b * used:(b + 1) * used], pad], axis=0))
    live = count[0]
    busy = lax.div(live + UNROLL - 1, UNROLL)

    def step(g, carry):
        tile_copy(g).wait()
        for u in range(UNROLL):
            k = g * UNROLL + u
            product = multiply(lhs[lax.rem(sources[k], blocks)], tiles[k])
            place = position_of(lax.rem(targets[k], HID_BLK), cube, streams)
            acc[place] += jnp.where(k < live, product, 0.0)
        return carry

    def drain(g, carry):
        tile_copy(g).wait()
        return carry

    lax.fori_loop(0, busy, step, 0)
    lax.fori_loop(busy, groups, drain, 0)
    half = cube // 2
    for s, stream in enumerate(streams):
        start, size = stream.first * cube, stream.units * half
        outs[2 * s][...] = acc[start + size:start + 2 * size]
        outs[2 * s + 1][...] = acc[start:start + size]


def fold_kernel(keep, came, send_out, keep_out):
    size = send_out.shape[0]
    send_out[...] = keep[size:] + came[size:]
    keep_out[...] = keep[:size] + came[:size]


def add_kernel(first, second, out):
    out[...] = first[...] + second[...]


def normalize_kernel(batch, channels, mine, other, gain, out):
    for i in range(out.shape[0]):
        total = mine[i] + other[i]
        row = lax.broadcasted_iota(jnp.int32, total.shape, 0)
        square = total * total
        scale = jnp.zeros_like(total)
        for n in range(batch):
            inside = lax.rem(row, batch) == n
            mean = jnp.sum(jnp.where(inside, square, 0.0), axis=0, keepdims=True) / channels
            scale = jnp.where(inside, lax.rsqrt(mean + EPSILON), scale)
        out[i] = total * gain[...] * scale


def join_kernel(first, second, out):
    size = first.shape[0]
    out[:size] = first[...]
    out[size:] = second[...]


def decode_kernel(cube, streams, count, targets, sources, tiles, *rest):
    hidden, out, lhs = rest[: 2 * len(streams)], rest[2 * len(streams)], rest[2 * len(streams) + 1]
    blocks = out.shape[0]
    half = cube // 2
    for s, stream in enumerate(streams):
        size = stream.units * half
        for part in range(2):
            for i in range(size):
                lhs[stream.first * cube + part * size + i] = block_rows(hidden[2 * s + part][i])
    out[...] = jnp.zeros_like(out)
    live = count[0]

    def step(g, carry):
        for u in range(UNROLL):
            k = g * UNROLL + u
            place = position_of(lax.rem(sources[k], HID_BLK), cube, streams)
            product = multiply(lhs[place], tiles[k])
            out[lax.rem(targets[k], blocks)] += jnp.where(k < live, product, 0.0)
        return carry

    lax.fori_loop(0, lax.div(live + UNROLL - 1, UNROLL), step, 0)


def finish_kernel(batch, field, mine, other, out, sums):
    blocks, _, width = mine.shape
    used = field.shape[0] // blocks
    square = jnp.zeros((used, width), jnp.float32)
    for b in range(blocks):
        total = (mine[b] + other[b])[:used]
        out[b * used:(b + 1) * used] = total
        error = total - field[b * used:(b + 1) * used]
        square = square + error * error
    high = lax.Precision.HIGHEST
    lanes = lax.dot_general(jnp.ones((8, width), jnp.float32), square, (((1,), (1,)), ((), ())),
                            precision=high, preferred_element_type=jnp.float32)
    row = lax.broadcasted_iota(jnp.int32, (used, width), 0)
    column = lax.broadcasted_iota(jnp.int32, (used, width), 1)
    pick = (lax.div(row, batch) == column).astype(jnp.float32)
    sums[...] = jnp.dot(lanes, pick, precision=high, preferred_element_type=jnp.float32)


def ORDER(depth, streams):
    return [(stage, s) for stage in range(2 * depth + 1) for s in range(streams)]


def flip(value, axes, partner, count):
    return lax.ppermute(value, axes, [(i, partner(i)) for i in range(count)])


def kernel(function, outs, scratch=(), specs=None):
    def call(*args):
        in_specs = specs or [IN_VMEM] * len(args)
        args = [pltpu.with_memory_space_constraint(a, pltpu.VMEM) if s is IN_VMEM else
                pltpu.with_memory_space_constraint(a, pltpu.HBM) if s is ANYWHERE else a
                for a, s in zip(args, in_specs)]
        return pl.pallas_call(
            function, out_shape=[pltpu.VMEM(o, jnp.float32) for o in outs], in_specs=in_specs,
            out_specs=[IN_VMEM] * len(outs), scratch_shapes=list(scratch),
            compiler_params=PARAMS)(*args)

    return call


def body(
    source_field,
    hidden_gain,
    enc_tiles,
    enc_src_block,
    enc_hid_block,
    enc_count,
    dec_tiles,
    dec_src_block,
    dec_hid_block,
    dec_count,
):
    src_blocks, batch, channels, width = source_field.shape
    n_src = lax.axis_size("src")
    n_hid = lax.axis_size("hid")
    levels = n_src.bit_length() - 1
    bits = list(range(levels - 1))
    cube = 1 << len(bits)
    half = cube // 2
    owned = HID_BLK // cube
    streams = make_streams(bits, owned)
    used = batch * channels
    rows = (used + 7) // 8 * 8
    slots = enc_tiles.shape[0]
    both = ("src", "hid")
    count = n_src * n_hid

    def swap(value, masks):
        def partner(i):
            src, hid = divmod(i, n_hid)
            return (src ^ masks[hid & 1]) * n_hid + hid

        return flip(value, both, partner, count)

    field = source_field.transpose(0, 2, 1, 3).reshape(src_blocks * used, width)
    gain = jnp.concatenate([jnp.repeat(hidden_gain, batch), jnp.zeros((rows - used,))])
    gain = jnp.broadcast_to(gain[:, None], (rows, width))

    pieces = kernel(
        functools.partial(encode_kernel, cube, streams),
        [(s.units * half, rows, width) for s in streams for _ in range(2)],
        specs=[IN_SMEM] + [ANYWHERE] * 4,
        scratch=[
            pltpu.SMEM((slots,), jnp.int32),
            pltpu.SMEM((slots,), jnp.int32),
            pltpu.VMEM((src_blocks * used, width), jnp.float32),
            pltpu.VMEM((slots, width, width), jnp.float32),
            pltpu.VMEM((src_blocks, rows, 2 * width), jnp.bfloat16),
            pltpu.VMEM((HID_BLK, rows, width), jnp.float32),
            pltpu.SemaphoreType.DMA((3,)),
            pltpu.SemaphoreType.DMA,
            pltpu.SemaphoreType.DMA((slots // UNROLL,)),
        ],
    )(enc_count, enc_src_block, enc_hid_block, field, enc_tiles)

    send = list(pieces[0::2])
    keep = list(pieces[1::2])
    hidden = [None] * len(streams)
    upper = [None] * len(streams)
    depth = len(bits)
    for stage, s in ORDER(depth, len(streams)):
        mask = (cube, cube) if stage == depth else tuple(
            1 << o[min(stage, 2 * depth - stage)] for o in streams[s].orders)
        if stage < depth:
            came = swap(send[s], mask)
            if stage + 1 < depth:
                size = keep[s].shape[0] // 2
                send[s], keep[s] = kernel(fold_kernel, [(size, rows, width)] * 2)(keep[s], came)
            else:
                [keep[s]] = kernel(add_kernel, [keep[s].shape])(keep[s], came)
        elif stage == depth:
            came = swap(keep[s], mask)
            [hidden[s]] = kernel(functools.partial(normalize_kernel, batch, channels), [keep[s].shape])(keep[s], came, gain)
        else:
            came = swap(hidden[s], mask)
            if stage < 2 * depth:
                [hidden[s]] = kernel(join_kernel, [(2 * hidden[s].shape[0], rows, width)])(
                    hidden[s], came)
            else:
                upper[s] = came

    [partial_back] = kernel(
        functools.partial(decode_kernel, cube, streams),
        [(src_blocks, rows, width)],
        specs=[IN_SMEM] * 3 + [IN_VMEM] * (1 + 2 * len(streams)),
        scratch=[pltpu.VMEM((HID_BLK, rows, 2 * width), jnp.bfloat16)],
    )(dec_count, dec_src_block, dec_hid_block, dec_tiles, *[x for pair in zip(hidden, upper) for x in pair])

    if n_hid == 2:
        others = flip(partial_back, "hid", lambda i: i ^ 1, n_hid)
    else:
        others = jnp.zeros_like(partial_back)
        partial_back = lax.psum(partial_back, "hid")
    returned, sums = kernel(
        functools.partial(finish_kernel, batch), [(src_blocks * used, width), (8, width)],
    )(field, partial_back, others)
    returned = returned.reshape(src_blocks, channels, batch, width).transpose(0, 2, 1, 3)

    for low in range(0, levels, 2):
        flips = [1 << low]
        if low + 1 < levels:
            flips += [2 << low, 3 << low]
        came = [flip(sums, "src", lambda i, mask=mask: i ^ mask, n_src) for mask in flips]
        sums = sums + came[0]
        if len(came) == 3:
            sums = sums + (came[1] + came[2])
    total_points = src_blocks * n_src * batch * width
    channel_rms = jnp.sqrt(sums[0, :channels] / total_points + EPSILON)
    return (returned, channel_rms)


def solution(mesh):
    in_specs = (
        P("src", None, None, None),
        P(),
        P(("src", "hid"), None, None),
        P(("src", "hid")),
        P(("src", "hid")),
        P(("src", "hid")),
        P(("src", "hid"), None, None),
        P(("src", "hid")),
        P(("src", "hid")),
        P(("src", "hid")),
    )
    out_specs = (P("src", None, None, None), P())
    return jax.shard_map(body, mesh=mesh, in_specs=in_specs, out_specs=out_specs, check_vma=False)
```

time: 278 us -> 98.2 us (0.35)
  waiting for transfers between devices: 169 us -> 48.4 us
  blocking collectives: 42 us -> 0 us
  starting transfers between devices: 0.08 us -> 37.5 us
  matrix products: 30 us -> 0 us
  between operations: 15.5 us -> 2.16 us
  other arithmetic: 12.4 us -> 0.53 us
  Pallas kernels: 0 us -> 8.21 us
  local copies, waits for them, and re-layouts: 7.89 us -> 1.22 us
    psum x2 -> x0, waiting for transfers between devices: 169 us -> none  [the longest x1 151 us: body(): lax.psum(partial_value, 'src')]
    ppermute x0 -> x35, waiting for transfers between devices: none -> 48.4 us  [flip(): return lax.ppermute(value, axes, [(i, partner(i)) for i in range(count)])]
    psum x1 -> x0, blocking collectives: 42 us -> none  [body(): sums = lax.psum(squares, 'src')]
    ppermute x0 -> x35, starting transfers between devices: none -> 37.5 us  [flip(): return lax.ppermute(value, axes, [(i, partner(i)) for i in range(count)])]
    dot_general x12 -> x0, matrix products: 30 us -> none  [the longest x2 6.31 us: encode_group(): product = jnp.einsum('tfr,trc->tfc', blocks, tiles, precision=HIGH)]
    pallas_call x0 -> x27, Pallas kernels: none -> 8.21 us  [call(): pl.pallas_call(function, out_shape=[pltpu.VMEM(o, jnp.float32) for o in o...]
    mul x2 -> x0, other arithmetic: 5.88 us -> none  [the longest x1 3.65 us: normalize(): mean_square = jnp.mean(grouped * grouped, axis=2, keepdims=True)]
    unnamed x12 -> x11, local copies, waits for them, and re-layouts: 5.07 us -> 0.92 us
  transfers between devices with their start and end apart: 2 -> 35, of which waited for: 2 -> 22; matrix products, arithmetic and copies ran while one was open for 0% -> 1% of each run, Pallas kernels for 0% -> 1%
where the time goes in v1:
time: 98.2 us; the launch traced here: 98 us
  waiting for transfers between devices  48.4 us (49%)
  starting transfers between devices  37.5 us (38%)
  Pallas kernels  8.21 us (8%)
  between operations  2.16 us (2%)
  local copies, waits for them, and re-layouts  1.22 us (1%)
    ppermute x35, waiting for transfers between devices, flip(): return lax.ppermute(value, axes, [(i, partner(i)) for i in range(count)])  48.4 us
    ppermute x35, starting transfers between devices, flip(): return lax.ppermute(value, axes, [(i, partner(i)) for i in range(count)])  37.5 us
    pallas_call x27, Pallas kernels, call(): pl.pallas_call(function, out_shape=[pltpu.VMEM(o, jnp.float32) for o in o...  8.21 us
  transfers between devices with their start and end apart: 35, of which 22 were waited for; matrix products, arithmetic and copies ran while one was open for 1% of the time, Pallas kernels for 1%

profile of v1, /device:TPU:0, one launch (start us, length us, event | category | flops | bytes accessed | tf_op | source)
XLA Modules:
  0.0 98.0 jit_solution(14020214827102590182)
XLA Ops:
  1.3 3.3 %shard_map.113 = (f32[4,200,128]{2,1,0:T(8,128)S(1)}, f32[4,200,128]{2,1,0:T(8,128)S(1)}, f32[4,200,128]{2,1,0:T(8,128)S(1)}, f32[4,200,128]{2,1,0:T(8,128)S(1)}...) custom-call(s32[1]{0:T(128)S(6)} %copy.13.count, ...), custom_call_target="tpu_custom_call" | custom-call | tf_op jit(solution)/shard_map/pallas_call | solution.py:210
  4.6 4.2 %collective-permute-start = (f32[4,200,128]{2,1,0:T(8,128)S(1)}, f32[4,200,128]{2,1,0:T(8,128)S(1)}, u32[]{:S(2)}, u32[]{:S(2)}) collective-permute-start(f32[4,200,128]{2,1,0:T(8,128)S(1)} %get-tuple-element.29), channel_id=1, source_target_pairs={{0,2},{1,3},{2,0},{3,1},{4,6},{5,7},{6,4},{7,5},{8,10},{9,11},{10,... | collective-permute-start | bytes 1228808 | tf_op jit(solution)/shard_map/ppermute | solution.py:201
  10.7 7.3 %collective-permute-done.came = f32[4,200,128]{2,1,0:T(8,128)S(1)} collective-permute-done((f32[4,200,128]{2,1,0:T(8,128)S(1)}, f32[4,200,128]{2,1,0:T(8,128)S(1)}, u32[]{:S(2)}, u32[]{:S(2)}) %collective-permute-start) | collective-permute-done | bytes 409632 | tf_op jit(solution)/shard_map/ppermute | solution.py:201
  18.1 3.0 %collective-permute-done.7.came = f32[4,200,128]{2,1,0:T(8,128)S(1)} collective-permute-done((f32[4,200,128]{2,1,0:T(8,128)S(1)}, f32[4,200,128]{2,1,0:T(8,128)S(1)}, u32[]{:S(2)}, u32[]{:S(2)}) %collective-permute-start.7) | collective-permute-done | bytes 409632 | tf_op jit(solution)/shard_map/ppermute | solution.py:201
  21.5 2.0 %collective-permute-done.21.came = f32[4,200,128]{2,1,0:T(8,128)S(1)} collective-permute-done((f32[4,200,128]{2,1,0:T(8,128)S(1)}, f32[4,200,128]{2,1,0:T(8,128)S(1)}, u32[]{:S(2)}, u32[]{:S(2)}) %collective-permute-start.21) | collective-permute-done | bytes 409632 | tf_op jit(solution)/shard_map/ppermute | solution.py:201
  23.6 2.4 %collective-permute-done.1.came = f32[2,200,128]{2,1,0:T(8,128)S(1)} collective-permute-done((f32[2,200,128]{2,1,0:T(8,128)S(1)}, f32[2,200,128]{2,1,0:T(8,128)S(1)}, u32[]{:S(2)}, u32[]{:S(2)}) %collective-permute-start.1) | collective-permute-done | bytes 204832 | tf_op jit(solution)/shard_map/ppermute | solution.py:201
  31.9 2.3 %collective-permute-start.3 = (f32[1,200,128]{2,1,0:T(8,128)S(1)}, f32[1,200,128]{2,1,0:T(8,128)S(1)}, u32[]{:S(2)}, u32[]{:S(2)}) collective-permute-start(f32[1,200,128]{2,1,0:T(8,128)S(1)} %shard_map.116.mine), channel_id=1, source_target_pairs={{0,16},{1,17},{2,18},{3,19},{4,20},{5,21},{6,22},{7,23},{8,24},{9,... | collective-permute-start | bytes 307208 | tf_op jit(solution)/shard_map/ppermute | solution.py:201
  34.2 1.7 %collective-permute-start.10 = (f32[1,200,128]{2,1,0:T(8,128)S(1)}, f32[1,200,128]{2,1,0:T(8,128)S(1)}, u32[]{:S(2)}, u32[]{:S(2)}) collective-permute-start(f32[1,200,128]{2,1,0:T(8,128)S(1)} %shard_map.122.mine), channel_id=1, source_target_pairs={{0,16},{1,17},{2,18},{3,19},{4,20},{5,21},{6,22},{7,23},{8,24},{9,... | collective-permute-start | bytes 307208 | tf_op jit(solution)/shard_map/ppermute | solution.py:201
  37.3 1.7 %collective-permute-start.24 = (f32[1,200,128]{2,1,0:T(8,128)S(1)}, f32[1,200,128]{2,1,0:T(8,128)S(1)}, u32[]{:S(2)}, u32[]{:S(2)}) collective-permute-start(f32[1,200,128]{2,1,0:T(8,128)S(1)} %shard_map.134.mine), channel_id=1, source_target_pairs={{0,16},{1,17},{2,18},{3,19},{4,20},{5,21},{6,22},{7,23},{8,24},{9,... | collective-permute-start | bytes 307208 | tf_op jit(solution)/shard_map/ppermute | solution.py:201
  39.2 7.7 %collective-permute-done.3.other = f32[1,200,128]{2,1,0:T(8,128)S(1)} collective-permute-done((f32[1,200,128]{2,1,0:T(8,128)S(1)}, f32[1,200,128]{2,1,0:T(8,128)S(1)}, u32[]{:S(2)}, u32[]{:S(2)}) %collective-permute-start.3) | collective-permute-done | bytes 102432 | tf_op jit(solution)/shard_map/ppermute | solution.py:201
  47.6 1.6 %collective-permute-done.10.other = f32[1,200,128]{2,1,0:T(8,128)S(1)} collective-permute-done((f32[1,200,128]{2,1,0:T(8,128)S(1)}, f32[1,200,128]{2,1,0:T(8,128)S(1)}, u32[]{:S(2)}, u32[]{:S(2)}) %collective-permute-start.10) | collective-permute-done | bytes 102432 | tf_op jit(solution)/shard_map/ppermute | solution.py:201
  49.2 2.1 %collective-permute-start.11 = (f32[1,200,128]{2,1,0:T(8,128)S(1)}, f32[1,200,128]{2,1,0:T(8,128)S(1)}, u32[]{:S(2)}, u32[]{:S(2)}) collective-permute-start(f32[1,200,128]{2,1,0:T(8,128)S(1)} %shard_map.123.first), channel_id=1, source_target_pairs={{0,2},{1,3},{2,0},{3,1},{4,6},{5,7},{6,4},{7,5},{8,10},{9,11},{10,... | collective-permute-start | bytes 307208 | tf_op jit(solution)/shard_map/ppermute | solution.py:201
  51.5 1.8 %collective-permute-start.18 = (f32[1,200,128]{2,1,0:T(8,128)S(1)}, f32[1,200,128]{2,1,0:T(8,128)S(1)}, u32[]{:S(2)}, u32[]{:S(2)}) collective-permute-start(f32[1,200,128]{2,1,0:T(8,128)S(1)} %shard_map.129.first), channel_id=1, source_target_pairs={{0,4},{1,5},{2,6},{3,7},{4,0},{5,1},{6,2},{7,3},{8,12},{9,13},{10,... | collective-permute-start | bytes 307208 | tf_op jit(solution)/shard_map/ppermute | solution.py:201
  54.1 2.1 %collective-permute-done.4.second = f32[1,200,128]{2,1,0:T(8,128)S(1)} collective-permute-done((f32[1,200,128]{2,1,0:T(8,128)S(1)}, f32[1,200,128]{2,1,0:T(8,128)S(1)}, u32[]{:S(2)}, u32[]{:S(2)}) %collective-permute-start.4) | collective-permute-done | bytes 102432 | tf_op jit(solution)/shard_map/ppermute | solution.py:201
  58.5 1.5 %collective-permute-start.26 = (f32[2,200,128]{2,1,0:T(8,128)S(1)}, f32[2,200,128]{2,1,0:T(8,128)S(1)}, u32[]{:S(2)}, u32[]{:S(2)}) collective-permute-start(f32[2,200,128]{2,1,0:T(8,128)S(1)} %shard_map.136.first), channel_id=1, source_target_pairs={{0,4},{1,9},{2,6},{3,11},{4,0},{5,13},{6,2},{7,15},{8,12},{9,1},{1... | collective-permute-start | bytes 614408 | tf_op jit(solution)/shard_map/ppermute | solution.py:201
  59.9 3.4 %collective-permute-done.5.second = f32[2,200,128]{2,1,0:T(8,128)S(1)} collective-permute-done((f32[2,200,128]{2,1,0:T(8,128)S(1)}, f32[2,200,128]{2,1,0:T(8,128)S(1)}, u32[]{:S(2)}, u32[]{:S(2)}) %collective-permute-start.5) | collective-permute-done | bytes 204832 | tf_op jit(solution)/shard_map/ppermute | solution.py:201
  69.2 4.9 %collective-permute-done.6.rest_1_ = f32[4,200,128]{2,1,0:T(8,128)S(1)} collective-permute-done((f32[4,200,128]{2,1,0:T(8,128)S(1)}, f32[4,200,128]{2,1,0:T(8,128)S(1)}, u32[]{:S(2)}, u32[]{:S(2)}) %collective-permute-start.6) | collective-permute-done | bytes 409632 | tf_op jit(solution)/shard_map/ppermute | solution.py:201
  74.1 3.7 %collective-permute-done.13.rest_3_ = f32[4,200,128]{2,1,0:T(8,128)S(1)} collective-permute-done((f32[4,200,128]{2,1,0:T(8,128)S(1)}, f32[4,200,128]{2,1,0:T(8,128)S(1)}, u32[]{:S(2)}, u32[]{:S(2)}) %collective-permute-start.13) | collective-permute-done | bytes 409632 | tf_op jit(solution)/shard_map/ppermute | solution.py:201
  78.5 3.4 %shard_map.138.mine = f32[8,200,128]{2,1,0:T(8,128)S(1)} custom-call(s32[1]{0:T(128)S(6)} %copy.14.count, s32[32]{0:T(128)S(1)} %copy-done.2, s32[32]{0:T(128)S(1)} %copy-done.3, f32[32,128,128]{2,1,0:T(8,128)S(1)} %copy-done.1, f32[4,200,128]{2,1,0:T(8,128)S(1)} %shard_map.119.rest_0_, f32[4,200,128]{2,1,0:T(8,128)S(1)} %collective-permute-done.6.rest_1_, ...), custom_call_target="tpu_custom_call" | custom-call | tf_op jit(solution)/shard_map/pallas_call | solution.py:210
  82.3 2.0 %collective-permute-done.28.other = f32[8,200,128]{2,1,0:T(8,128)S(1)} collective-permute-done((f32[8,200,128]{2,1,0:T(8,128)S(1)}, f32[8,200,128]{2,1,0:T(8,128)S(1)}, u32[]{:S(2)}, u32[]{:S(2)}) %collective-permute-start.28) | collective-permute-done | bytes 819232 | tf_op jit(solution)/shard_map/ppermute | solution.py:201
  85.0 1.9 %collective-permute-start.30 = (f32[8,128]{1,0:T(8,128)S(1)}, f32[8,128]{1,0:T(8,128)S(1)}, u32[]{:S(2)}, u32[]{:S(2)}) collective-permute-start(f32[8,128]{1,0:T(8,128)S(1)} %get-tuple-element.53), channel_id=1, source_target_pairs={{0,4},{2,6},{4,0},{6,2},{8,12},{10,14},{12,8},{14,10},{16,20},{18,... | collective-permute-start | bytes 12296 | tf_op jit(solution)/shard_map/ppermute | solution.py:201
  86.9 1.6 %collective-permute-start.29 = (f32[8,128]{1,0:T(8,128)S(1)}, f32[8,128]{1,0:T(8,128)S(1)}, u32[]{:S(2)}, u32[]{:S(2)}) collective-permute-start(f32[8,128]{1,0:T(8,128)S(1)} %get-tuple-element.53), channel_id=1, source_target_pairs={{0,2},{2,0},{4,6},{6,4},{8,10},{10,8},{12,14},{14,12},{16,18},{18,... | collective-permute-start | bytes 12296 | tf_op jit(solution)/shard_map/ppermute | solution.py:201
  90.5 2.5 %collective-permute-start.34 = (f32[8,128]{1,0:T(8,128)S(1)}, f32[8,128]{1,0:T(8,128)S(1)}, u32[]{:S(2)}, u32[]{:S(2)}) collective-permute-start(f32[8,128]{1,0:T(8,128)S(1)} %add_add_fusion.1), channel_id=1, source_target_pairs={{0,24},{2,26},{4,28},{6,30},{8,16},{10,18},{12,20},{14,22},{16,8},... | collective-permute-start | bytes 12296 | tf_op jit(solution)/shard_map/ppermute | solution.py:201
  95.9 1.6 %collective-permute-done.33 = f32[8,128]{1,0:T(8,128)S(1)} collective-permute-done((f32[8,128]{1,0:T(8,128)S(1)}, f32[8,128]{1,0:T(8,128)S(1)}, u32[]{:S(2)}, u32[]{:S(2)}) %collective-permute-start.33) | collective-permute-done | bytes 4128 | tf_op jit(solution)/shard_map/ppermute | solution.py:201
  (91 shorter events, 26.4 us)
Async XLA Ops:
  4.6 13.3 %collective-permute-start = (f32[4,200,128]{2,1,0:T(8,128)S(1)}, f32[4,200,128]{2,1,0:T(8,128)S(1)}, u32[]{:S(2)}, u32[]{:S(2)}) collective-permute-start(f32[4,200,128]{2,1,0:T(8,128)S(1)} %get-tuple-element.29), channel_id=1, source_target_pairs={{0,2},{1,3},{2,0},{3,1},{4,6},{5,7},{6,4},{7,5},{8,10},{9,11},{10,... | collective-permute-start | bytes 1228808 | tf_op jit(solution)/shard_map/ppermute | solution.py:201
  8.8 12.3 %collective-permute-start.7 = (f32[4,200,128]{2,1,0:T(8,128)S(1)}, f32[4,200,128]{2,1,0:T(8,128)S(1)}, u32[]{:S(2)}, u32[]{:S(2)}) collective-permute-start(f32[4,200,128]{2,1,0:T(8,128)S(1)} %get-tuple-element.35), channel_id=1, source_target_pairs={{0,4},{1,5},{2,6},{3,7},{4,0},{5,1},{6,2},{7,3},{8,12},{9,13},{10,... | collective-permute-start | bytes 1228808 | tf_op jit(solution)/shard_map/ppermute | solution.py:201
  8.8 12.5 %collective-permute-start.14 = (f32[4,200,128]{2,1,0:T(8,128)S(1)}, f32[4,200,128]{2,1,0:T(8,128)S(1)}, u32[]{:S(2)}, u32[]{:S(2)}) collective-permute-start(f32[4,200,128]{2,1,0:T(8,128)S(1)} %get-tuple-element.41), channel_id=1, source_target_pairs={{0,8},{1,9},{2,10},{3,11},{4,12},{5,13},{6,14},{7,15},{8,0},{9,1},... | collective-permute-start | bytes 1228808 | tf_op jit(solution)/shard_map/ppermute | solution.py:201
  9.9 13.6 %collective-permute-start.21 = (f32[4,200,128]{2,1,0:T(8,128)S(1)}, f32[4,200,128]{2,1,0:T(8,128)S(1)}, u32[]{:S(2)}, u32[]{:S(2)}) collective-permute-start(f32[4,200,128]{2,1,0:T(8,128)S(1)} %get-tuple-element.47), channel_id=1, source_target_pairs={{0,2},{1,5},{2,0},{3,7},{4,6},{5,1},{6,4},{7,3},{8,10},{9,13},{10,... | collective-permute-start | bytes 1228808 | tf_op jit(solution)/shard_map/ppermute | solution.py:201
  18.0 8.0 %collective-permute-start.1 = (f32[2,200,128]{2,1,0:T(8,128)S(1)}, f32[2,200,128]{2,1,0:T(8,128)S(1)}, u32[]{:S(2)}, u32[]{:S(2)}) collective-permute-start(f32[2,200,128]{2,1,0:T(8,128)S(1)} %get-tuple-element.31), channel_id=1, source_target_pairs={{0,4},{1,5},{2,6},{3,7},{4,0},{5,1},{6,2},{7,3},{8,12},{9,13},{10,... | collective-permute-start | bytes 614408 | tf_op jit(solution)/shard_map/ppermute | solution.py:201
  21.3 6.7 %collective-permute-start.15 = (f32[2,200,128]{2,1,0:T(8,128)S(1)}, f32[2,200,128]{2,1,0:T(8,128)S(1)}, u32[]{:S(2)}, u32[]{:S(2)}) collective-permute-start(f32[2,200,128]{2,1,0:T(8,128)S(1)} %get-tuple-element.43), channel_id=1, source_target_pairs={{0,2},{1,3},{2,0},{3,1},{4,6},{5,7},{6,4},{7,5},{8,10},{9,11},{10,... | collective-permute-start | bytes 614408 | tf_op jit(solution)/shard_map/ppermute | solution.py:201
  23.5 6.9 %collective-permute-start.22 = (f32[2,200,128]{2,1,0:T(8,128)S(1)}, f32[2,200,128]{2,1,0:T(8,128)S(1)}, u32[]{:S(2)}, u32[]{:S(2)}) collective-permute-start(f32[2,200,128]{2,1,0:T(8,128)S(1)} %get-tuple-element.49), channel_id=1, source_target_pairs={{0,4},{1,9},{2,6},{3,11},{4,0},{5,13},{6,2},{7,15},{8,12},{9,1},{1... | collective-permute-start | bytes 614408 | tf_op jit(solution)/shard_map/ppermute | solution.py:201
  27.0 7.2 %collective-permute-start.9 = (f32[1,200,128]{2,1,0:T(8,128)S(1)}, f32[1,200,128]{2,1,0:T(8,128)S(1)}, u32[]{:S(2)}, u32[]{:S(2)}) collective-permute-start(f32[1,200,128]{2,1,0:T(8,128)S(1)} %get-tuple-element.39), channel_id=1, source_target_pairs={{0,2},{1,3},{2,0},{3,1},{4,6},{5,7},{6,4},{7,5},{8,10},{9,11},{10,... | collective-permute-start | bytes 307208 | tf_op jit(solution)/shard_map/ppermute | solution.py:201
  28.0 7.9 %collective-permute-start.16 = (f32[1,200,128]{2,1,0:T(8,128)S(1)}, f32[1,200,128]{2,1,0:T(8,128)S(1)}, u32[]{:S(2)}, u32[]{:S(2)}) collective-permute-start(f32[1,200,128]{2,1,0:T(8,128)S(1)} %get-tuple-element.45), channel_id=1, source_target_pairs={{0,4},{1,5},{2,6},{3,7},{4,0},{5,1},{6,2},{7,3},{8,12},{9,13},{10,... | collective-permute-start | bytes 307208 | tf_op jit(solution)/shard_map/ppermute | solution.py:201
  30.4 6.9 %collective-permute-start.23 = (f32[1,200,128]{2,1,0:T(8,128)S(1)}, f32[1,200,128]{2,1,0:T(8,128)S(1)}, u32[]{:S(2)}, u32[]{:S(2)}) collective-permute-start(f32[1,200,128]{2,1,0:T(8,128)S(1)} %get-tuple-element.51), channel_id=1, source_target_pairs={{0,8},{1,3},{2,10},{3,1},{4,12},{5,7},{6,14},{7,5},{8,0},{9,11},{1... | collective-permute-start | bytes 307208 | tf_op jit(solution)/shard_map/ppermute | solution.py:201
  31.9 15.1 %collective-permute-start.3 = (f32[1,200,128]{2,1,0:T(8,128)S(1)}, f32[1,200,128]{2,1,0:T(8,128)S(1)}, u32[]{:S(2)}, u32[]{:S(2)}) collective-permute-start(f32[1,200,128]{2,1,0:T(8,128)S(1)} %shard_map.116.mine), channel_id=1, source_target_pairs={{0,16},{1,17},{2,18},{3,19},{4,20},{5,21},{6,22},{7,23},{8,24},{9,... | collective-permute-start | bytes 307208 | tf_op jit(solution)/shard_map/ppermute | solution.py:201
  34.2 15.0 %collective-permute-start.10 = (f32[1,200,128]{2,1,0:T(8,128)S(1)}, f32[1,200,128]{2,1,0:T(8,128)S(1)}, u32[]{:S(2)}, u32[]{:S(2)}) collective-permute-start(f32[1,200,128]{2,1,0:T(8,128)S(1)} %shard_map.122.mine), channel_id=1, source_target_pairs={{0,16},{1,17},{2,18},{3,19},{4,20},{5,21},{6,22},{7,23},{8,24},{9,... | collective-permute-start | bytes 307208 | tf_op jit(solution)/shard_map/ppermute | solution.py:201
  35.9 15.5 %collective-permute-start.17 = (f32[1,200,128]{2,1,0:T(8,128)S(1)}, f32[1,200,128]{2,1,0:T(8,128)S(1)}, u32[]{:S(2)}, u32[]{:S(2)}) collective-permute-start(f32[1,200,128]{2,1,0:T(8,128)S(1)} %shard_map.128.mine), channel_id=1, source_target_pairs={{0,16},{1,17},{2,18},{3,19},{4,20},{5,21},{6,22},{7,23},{8,24},{9,... | collective-permute-start | bytes 307208 | tf_op jit(solution)/shard_map/ppermute | solution.py:201
  37.3 16.4 %collective-permute-start.24 = (f32[1,200,128]{2,1,0:T(8,128)S(1)}, f32[1,200,128]{2,1,0:T(8,128)S(1)}, u32[]{:S(2)}, u32[]{:S(2)}) collective-permute-start(f32[1,200,128]{2,1,0:T(8,128)S(1)} %shard_map.134.mine), channel_id=1, source_target_pairs={{0,16},{1,17},{2,18},{3,19},{4,20},{5,21},{6,22},{7,23},{8,24},{9,... | collective-permute-start | bytes 307208 | tf_op jit(solution)/shard_map/ppermute | solution.py:201
  47.1 9.0 %collective-permute-start.4 = (f32[1,200,128]{2,1,0:T(8,128)S(1)}, f32[1,200,128]{2,1,0:T(8,128)S(1)}, u32[]{:S(2)}, u32[]{:S(2)}) collective-permute-start(f32[1,200,128]{2,1,0:T(8,128)S(1)} %shard_map.117.first), channel_id=1, source_target_pairs={{0,8},{1,9},{2,10},{3,11},{4,12},{5,13},{6,14},{7,15},{8,0},{9,1},... | collective-permute-start | bytes 307208 | tf_op jit(solution)/shard_map/ppermute | solution.py:201
  49.2 8.0 %collective-permute-start.11 = (f32[1,200,128]{2,1,0:T(8,128)S(1)}, f32[1,200,128]{2,1,0:T(8,128)S(1)}, u32[]{:S(2)}, u32[]{:S(2)}) collective-permute-start(f32[1,200,128]{2,1,0:T(8,128)S(1)} %shard_map.123.first), channel_id=1, source_target_pairs={{0,2},{1,3},{2,0},{3,1},{4,6},{5,7},{6,4},{7,5},{8,10},{9,11},{10,... | collective-permute-start | bytes 307208 | tf_op jit(solution)/shard_map/ppermute | solution.py:201
  56.2 7.2 %collective-permute-start.5 = (f32[2,200,128]{2,1,0:T(8,128)S(1)}, f32[2,200,128]{2,1,0:T(8,128)S(1)}, u32[]{:S(2)}, u32[]{:S(2)}) collective-permute-start(f32[2,200,128]{2,1,0:T(8,128)S(1)} %shard_map.118.first), channel_id=1, source_target_pairs={{0,4},{1,5},{2,6},{3,7},{4,0},{5,1},{6,2},{7,3},{8,12},{9,13},{10,... | collective-permute-start | bytes 614408 | tf_op jit(solution)/shard_map/ppermute | solution.py:201
  57.3 8.0 %collective-permute-start.12 = (f32[2,200,128]{2,1,0:T(8,128)S(1)}, f32[2,200,128]{2,1,0:T(8,128)S(1)}, u32[]{:S(2)}, u32[]{:S(2)}) collective-permute-start(f32[2,200,128]{2,1,0:T(8,128)S(1)} %shard_map.124.first), channel_id=1, source_target_pairs={{0,8},{1,9},{2,10},{3,11},{4,12},{5,13},{6,14},{7,15},{8,0},{9,1},... | collective-permute-start | bytes 614408 | tf_op jit(solution)/shard_map/ppermute | solution.py:201
  57.4 9.0 %collective-permute-start.19 = (f32[2,200,128]{2,1,0:T(8,128)S(1)}, f32[2,200,128]{2,1,0:T(8,128)S(1)}, u32[]{:S(2)}, u32[]{:S(2)}) collective-permute-start(f32[2,200,128]{2,1,0:T(8,128)S(1)} %shard_map.130.first), channel_id=1, source_target_pairs={{0,2},{1,3},{2,0},{3,1},{4,6},{5,7},{6,4},{7,5},{8,10},{9,11},{10,... | collective-permute-start | bytes 614408 | tf_op jit(solution)/shard_map/ppermute | solution.py:201
  58.5 8.7 %collective-permute-start.26 = (f32[2,200,128]{2,1,0:T(8,128)S(1)}, f32[2,200,128]{2,1,0:T(8,128)S(1)}, u32[]{:S(2)}, u32[]{:S(2)}) collective-permute-start(f32[2,200,128]{2,1,0:T(8,128)S(1)} %shard_map.136.first), channel_id=1, source_target_pairs={{0,4},{1,9},{2,6},{3,11},{4,0},{5,13},{6,2},{7,15},{8,12},{9,1},{1... | collective-permute-start | bytes 614408 | tf_op jit(solution)/shard_map/ppermute | solution.py:201
  63.4 10.7 %collective-permute-start.6 = (f32[4,200,128]{2,1,0:T(8,128)S(1)}, f32[4,200,128]{2,1,0:T(8,128)S(1)}, u32[]{:S(2)}, u32[]{:S(2)}) collective-permute-start(f32[4,200,128]{2,1,0:T(8,128)S(1)} %shard_map.119.rest_0_), channel_id=1, source_target_pairs={{0,2},{1,3},{2,0},{3,1},{4,6},{5,7},{6,4},{7,5},{8,10},{9,11},{10,... | collective-permute-start | bytes 1228808 | tf_op jit(solution)/shard_map/ppermute | solution.py:201
  65.3 12.4 %collective-permute-start.13 = (f32[4,200,128]{2,1,0:T(8,128)S(1)}, f32[4,200,128]{2,1,0:T(8,128)S(1)}, u32[]{:S(2)}, u32[]{:S(2)}) collective-permute-start(f32[4,200,128]{2,1,0:T(8,128)S(1)} %shard_map.125.rest_2_), channel_id=1, source_target_pairs={{0,4},{1,5},{2,6},{3,7},{4,0},{5,1},{6,2},{7,3},{8,12},{9,13},{10,... | collective-permute-start | bytes 1228808 | tf_op jit(solution)/shard_map/ppermute | solution.py:201
  66.5 11.3 %collective-permute-start.20 = (f32[4,200,128]{2,1,0:T(8,128)S(1)}, f32[4,200,128]{2,1,0:T(8,128)S(1)}, u32[]{:S(2)}, u32[]{:S(2)}) collective-permute-start(f32[4,200,128]{2,1,0:T(8,128)S(1)} %shard_map.131.rest_4_), channel_id=1, source_target_pairs={{0,8},{1,9},{2,10},{3,11},{4,12},{5,13},{6,14},{7,15},{8,0},{9,1},... | collective-permute-start | bytes 1228808 | tf_op jit(solution)/shard_map/ppermute | solution.py:201
  67.2 11.2 %collective-permute-start.27 = (f32[4,200,128]{2,1,0:T(8,128)S(1)}, f32[4,200,128]{2,1,0:T(8,128)S(1)}, u32[]{:S(2)}, u32[]{:S(2)}) collective-permute-start(f32[4,200,128]{2,1,0:T(8,128)S(1)} %shard_map.137.rest_6_), channel_id=1, source_target_pairs={{0,2},{1,5},{2,0},{3,7},{4,6},{5,1},{6,4},{7,3},{8,10},{9,13},{10,... | collective-permute-start | bytes 1228808 | tf_op jit(solution)/shard_map/ppermute | solution.py:201
  (16 other events, 147.3 us)
